TPU v7x, 32 devices: a whole 2x2x4 slice. The times are simulated.
32 devices in a mesh: lat: 8 (over z, core), lon: 4 (over y, x).
Axes of the slice: x: 2, y: 2, z: 4, core: 2. Of those that a mesh axis runs over, the one named last changes fastest.
Arguments:
- field: bfloat16 [128, 128, 256], P('lat', 'lon'), may hold values from -6 to 6
- weights: bfloat16 [8, 4, 3072, 3072], P('lat', 'lon'), may hold values from -0.09375 to 0.09375
- strip_ids: int32 [8, 8], P('lat'), may hold values from 0 to 31, as said below
- counts: int32 [8], P('lat'), may hold values from 2 to 8, as said below
Outputs:
- remapped: bfloat16 [32768, 256], P(('lat', 'lon'))
Inputs may be any that keep to these rules, and one draw needn't show every extreme that they name: `strip_ids`: row b holds consecutive global strip numbers, the last one repeated where the run meets the end of its window, all among the strips of source bands b - 2 to b + 2, band c holding strips 4 * c to 4 * c + 3. Band b uses the first counts[b] slots of its row.
All inputs are finite; a program needn't handle non-finite values.
Results may differ from a plain program's by a relative error of at most 0.0059.
Values may be sent and summed in bfloat16 or wider, within the bound.
A program may use at most 64 MiB of HBM per device.

v0:
```python
import functools

import jax
import jax.numpy as jnp
from jax import lax
from jax.experimental import pallas as pl
from jax.experimental.pallas import tpu as pltpu
from jax.sharding import PartitionSpec as P

STRIP_ROWS = 4
REACH = 2
LANES = 128
CHUNKS = 4
MESH = pl.DeviceIdType.MESH
F32 = jnp.float32
BF16 = jnp.bfloat16


def kernel(
    n_lat, n_lon, field, weights, ids, counts, out,
    win, ghost, edge, wv, picked, near, own, out_a, out_b, in_a, in_b,
    w_sem, own_sem, tile_send, tile_recv, fwd_send, row_send, row_recv,
    edge_send, edge_recv, a_send, a_recv, b_send, b_recv,
):
    b = lax.axis_index("lat")
    s = lax.axis_index("lon")
    rows, lons, chans = field.shape
    halves = chans // LANES
    slots = ids.shape[1]
    third = weights.shape[2] // 3
    part = third // CHUNKS
    odd = lax.rem(b, 2)
    partner = b + 1 - 2 * odd
    s_odd = lax.rem(s, 2)
    bands = 2 * REACH + 1

    def lon_at(step):
        return lax.rem(s + step + n_lon, n_lon)

    def valid(band):
        return jnp.logical_and(band >= 0, band < n_lat)

    def place(offset):
        return (offset + REACH) * rows + 1

    def lanes(h):
        return pl.ds(h * LANES, LANES)

    far_row = 2 * third * s_odd
    near_row = 2 * third * (1 - s_odd)
    far_to = lax.rem(s + n_lon - 2 + 4 * s_odd, n_lon)
    near_to = lax.rem(s + n_lon + 1 - 2 * s_odd, n_lon)

    loads = []
    for i, start in enumerate((far_row, near_row, third)):
        span = pl.ds(pl.multiple_of(start, third), third)
        loads.append(pltpu.make_async_copy(weights.at[0, 0, span], wv.at[span], w_sem.at[i]))
    own_loads = [
        pltpu.make_async_copy(field.at[:, :, lanes(h)], win[h].at[pl.ds(place(0), rows)], own_sem.at[h])
        for h in range(halves)
    ]
    for copy in own_loads:
        copy.start()

    barrier = pltpu.get_barrier_semaphore()
    expected = 0

    def greet(band, sector):
        pl.semaphore_signal(barrier, inc=1, device_id=(band, sector), device_id_type=MESH)

    greet(partner, s)
    greet(b, lon_at(-2))
    greet(b, lon_at(2))
    expected = 3
    for offset in range(-REACH - 1, REACH + 2):
        if abs(offset) >= 2:
            @pl.when(valid(b + offset))
            def _():
                greet(b + offset, s)
            expected = expected + valid(b + offset).astype(jnp.int32)
        if abs(offset) <= REACH:
            @pl.when(valid(b + offset))
            def _():
                greet(b + offset, lon_at(-1))
                greet(b + offset, lon_at(1))
            expected = expected + 2 * valid(b + offset).astype(jnp.int32)

    loads[0].start()
    for copy in own_loads:
        copy.wait()
    for h in range(halves):
        for r in range(rows):
            cells = win[h][place(0) + r].astype(F32)
            edge[0, h, r] = cells[lons - 1 :]
            edge[1, h, r] = cells[:1]
    pl.semaphore_wait(barrier, expected)

    def remote(src, dst, send, recv, band, sector):
        return pltpu.make_async_remote_copy(
            src_ref=src, dst_ref=dst, send_sem=send, recv_sem=recv,
            device_id=(band, sector), device_id_type=MESH,
        )

    def tile_copy(kind, h):
        delta = (partner - b, REACH, -REACH)[kind]
        return remote(
            win[h].at[pl.ds(place(0), rows)], win[h].at[pl.ds(place(-delta), rows)],
            tile_send.at[kind, h], tile_recv.at[kind, h], b + delta, s,
        )

    def forward_copy(h):
        offset = REACH - 2 * REACH * odd
        return remote(
            win[h].at[pl.ds(place(offset), rows)], win[h].at[pl.ds(place(offset + b - partner), rows)],
            fwd_send.at[h], tile_recv.at[3, h], partner, s,
        )

    def row_copy(kind, h):
        if kind == 0:
            src, dst, band = field.at[pl.ds(rows - 1, 1), :, lanes(h)], win[h].at[pl.ds(0, 1)], b + REACH + 1
        else:
            src, dst, band = field.at[pl.ds(0, 1), :, lanes(h)], win[h].at[pl.ds(bands * rows + 1, 1)], b - REACH - 1
        return remote(src, dst, row_send.at[kind, h], row_recv.at[kind, h], band, s)

    def edge_copy(side, offset):
        return remote(
            edge.at[side], ghost.at[side, :, pl.ds((REACH - offset) * rows, rows)],
            edge_send.at[side, offset + REACH], edge_recv.at[side, REACH - offset],
            b + offset, lon_at(1 - 2 * side),
        )

    def each_tile(h, act):
        act(tile_copy(0, h))
        for kind, delta in ((1, REACH), (2, -REACH)):
            @pl.when(valid(b + delta))
            def _():
                act(tile_copy(kind, h))

    def each_row(h, act):
        for kind, delta in ((0, REACH + 1), (1, -REACH - 1)):
            @pl.when(valid(b + delta))
            def _():
                act(row_copy(kind, h))

    def each_edge(act):
        for offset in range(-REACH, REACH + 1):
            @pl.when(valid(b + offset))
            def _():
                for side in range(2):
                    act(edge_copy(side, offset))

    each_edge(lambda copy: copy.start())
    for h in range(halves):
        each_row(h, lambda copy: copy.start())
        each_tile(h, lambda copy: copy.start())
    loads[1].start()
    loads[2].start()

    forwards = valid(b + REACH - 2 * REACH * odd)
    receives = valid(b - 1 + 2 * odd)

    def pass_on(h):
        @pl.when(valid(b - REACH))
        def _():
            tile_copy(1, h).wait_recv()

        @pl.when(valid(b + REACH))
        def _():
            tile_copy(2, h).wait_recv()

        @pl.when(forwards)
        def _():
            forward_copy(h).start()

    def settle(h):
        tile_copy(0, h).wait_recv()

        @pl.when(valid(b - REACH - 1))
        def _():
            row_copy(0, h).wait_recv()

        @pl.when(valid(b + REACH + 1))
        def _():
            row_copy(1, h).wait_recv()

        if h == 0:
            for offset in range(-REACH, REACH + 1):
                @pl.when(valid(b + offset))
                def _():
                    for side in range(2):
                        edge_copy(side, -offset).wait_recv()

        @pl.when(receives)
        def _():
            forward_copy(h).wait_recv()

    first_row = place(0) - b * rows
    last_row = first_row + n_lat * rows - 1
    cell = lax.broadcasted_iota(jnp.int32, (lons, LANES), 0)
    depth = STRIP_ROWS * lons
    live_count = counts[0]

    def pick(h):
        for k in range(slots):
            live = jnp.full((lons, LANES), k < live_count)
            start = ids[0, k] * STRIP_ROWS + first_row
            for j in range(STRIP_ROWS):
                at = jnp.clip(start + j, 1, bands * rows)
                centre = win[h][at].astype(F32)
                above = win[h][jnp.maximum(at - 1, first_row)].astype(F32)
                below = win[h][jnp.minimum(at + 1, last_row)].astype(F32)
                west = jnp.where(cell == 0, ghost[0, h, at - 1], pltpu.roll(centre, 1, 0))
                east = jnp.where(cell == lons - 1, ghost[1, h, at - 1], pltpu.roll(centre, lons - 1, 0))
                for c, value in enumerate((centre, (east - west) * 0.5, (below - above) * 0.5)):
                    span = pl.ds((3 * k + c) * depth + j * lons, lons)
                    picked[h, span, :] = jnp.where(live, value, 0.0).astype(BF16)

    def product(h, start, i):
        span = pl.ds(pl.multiple_of(start + i * part, part), part)
        return jnp.dot(wv[span, :], picked[h], preferred_element_type=F32)

    def a_copy(h, i):
        return remote(out_a.at[h, i], in_a.at[h, i], a_send.at[h, i], a_recv.at[h, i], b, far_to)

    def b_copy(h, i):
        return remote(out_b.at[h, i], in_b.at[h, i], b_send.at[h, i], b_recv.at[h, i], b, near_to)

    def far(h, i):
        out_a[h, i] = product(h, far_row, i).astype(BF16)
        a_copy(h, i).start()

    def relay(h, i):
        a_copy(h, i).wait_recv()
        out_b[h, i] = (near[h, i] + in_a[h, i].astype(F32)).astype(BF16)
        b_copy(h, i).start()

    def finish(h, i):
        b_copy(h, i).wait_recv()
        span = pl.ds(pl.multiple_of(i * part, part), part)
        out[span, lanes(h)] = (own[h, i] + in_b[h, i].astype(F32)).astype(BF16)

    def steps(act):
        def step(i, carry):
            act(i)
            return carry
        lax.fori_loop(0, CHUNKS, step, 0)

    def near_step(h):
        def act(i):
            near[h, i] = product(h, near_row, i)
        return act

    def far_and_relay(i):
        far(1, i)
        relay(0, i)

    def own_and_relay(i):
        own[0, i] = product(0, third, i)
        relay(1, i)

    def own_and_finish(i):
        own[1, i] = product(1, third, i)
        finish(0, i)

    pass_on(0)
    settle(0)
    pick(0)
    loads[0].wait()
    steps(functools.partial(far, 0))
    pass_on(1)
    loads[1].wait()
    steps(near_step(0))
    settle(1)
    pick(1)
    steps(far_and_relay)
    steps(near_step(1))
    loads[2].wait()
    steps(own_and_relay)
    steps(own_and_finish)
    steps(functools.partial(finish, 1))

    each_edge(lambda copy: copy.wait_send())
    for h in range(halves):
        each_row(h, lambda copy: copy.wait_send())
        each_tile(h, lambda copy: copy.wait_send())

        @pl.when(forwards)
        def _():
            forward_copy(h).wait_send()

        for i in range(CHUNKS):
            a_copy(h, i).wait_send()
            b_copy(h, i).wait_send()


def solution(mesh):
    n_lat, n_lon = mesh.shape["lat"], mesh.shape["lon"]

    def body(field, weights, strip_ids, counts):
        rows, lons, chans = field.shape
        tall, wide = weights.shape[2:]
        third = tall // 3
        part = third // CHUNKS
        halves = chans // LANES
        bands = 2 * REACH + 1
        dma = pltpu.SemaphoreType.DMA
        block = (halves, CHUNKS, part, LANES)
        return pl.pallas_call(
            functools.partial(kernel, n_lat, n_lon),
            out_shape=pltpu.VMEM((third, chans), BF16),
            in_specs=[
                pl.BlockSpec(memory_space=pl.ANY),
                pl.BlockSpec(memory_space=pl.ANY),
                pl.BlockSpec(memory_space=pltpu.SMEM),
                pl.BlockSpec(memory_space=pltpu.SMEM),
            ],
            out_specs=pl.BlockSpec(memory_space=pltpu.VMEM),
            scratch_shapes=[
                [pltpu.VMEM((bands * rows + 2, lons, LANES), BF16) for _ in range(halves)],
                pltpu.VMEM((2, halves, bands * rows, 1, LANES), F32),
                pltpu.VMEM((2, halves, rows, 1, LANES), F32),
                pltpu.VMEM((tall, wide), BF16),
                pltpu.VMEM((halves, wide, LANES), BF16),
                pltpu.VMEM(block, F32),
                pltpu.VMEM(block, F32),
                pltpu.VMEM(block, BF16),
                pltpu.VMEM(block, BF16),
                pltpu.VMEM(block, BF16),
                pltpu.VMEM(block, BF16),
                dma((3,)),
                dma((halves,)),
                dma((3, halves)),
                dma((4, halves)),
                dma((halves,)),
                dma((2, halves)),
                dma((2, halves)),
                dma((2, bands)),
                dma((2, bands)),
                dma((halves, CHUNKS)),
                dma((halves, CHUNKS)),
                dma((halves, CHUNKS)),
                dma((halves, CHUNKS)),
            ],
            compiler_params=pltpu.CompilerParams(collective_id=0, has_side_effects=True),
        )(field, weights, strip_ids, counts)

    placed = (P("lat", "lon", None), P("lat", "lon", None, None), P("lat", None), P("lat"))
    return jax.shard_map(
        body, mesh=mesh, in_specs=placed, out_specs=P(("lat", "lon"), None), check_vma=False
    )
```

profile of v0, /device:TPU:0, one launch (start us, length us, event | category | flops | bytes accessed | tf_op | source)
XLA Modules:
  0.0 33.7 jit_solution(6550732553013566101)
XLA Ops:
  0.7 32.2 %shard_map.46 = bf16[1024,256]{1,0:T(8,128)(2,1)S(1)} custom-call(bf16[16,32,256]{2,1,0:T(8,128)(2,1)} %field.1, bf16[1,1,3072,3072]{3,2,1,0:T(8,128)(2,1)} %weights.1, s32[1,8]{1,0:T(1,128)} %ids.1, s32[1]{0:T(128)S(6)} %copy.7.counts), custom_call_target="tpu_custom_call" | custom-call | tf_op jit(solution)/shard_map/pallas_call | solution.py:308
  32.9 0.8 %copy.6 = bf16[1024,256]{1,0:T(8,128)(2,1)} copy(bf16[1024,256]{1,0:T(8,128)(2,1)S(1)} %shard_map.46) | data formatting | bytes 1048576
where the time goes:
time: 33.8 us; the launch traced here: 33.7 us
  Pallas kernels  32.2 us (95%)
  local copies, waits for them, and re-layouts  0.8 us (2%)
  between operations  0.66 us (2%)
    pallas_call x1, Pallas kernels, body(): pl.pallas_call(functools.partial(kernel, n_lat, n_lon), out_shape=pltpu.V...  32.2 us
    unnamed x1, local copies, waits for them, and re-layouts  0.8 us

commit v1 on v0

v1 whole, which is shorter than its diff:
```python
import functools

import jax
import jax.numpy as jnp
from jax import lax
from jax.experimental import pallas as pl
from jax.experimental.pallas import tpu as pltpu
from jax.sharding import PartitionSpec as P

STRIP_ROWS = 4
REACH = 2
LANES = 128
CHUNKS = 4
SUB = 2
PIECES = CHUNKS * SUB
MESH = pl.DeviceIdType.MESH
F32 = jnp.float32
BF16 = jnp.bfloat16


def kernel(
    n_lat, n_lon, field, weights, ids_hbm, counts_hbm, out,
    ids, counts, win, edge_f, edge, relayed, ghost, ghost_f, wv, picked, near, own, out_a, out_b, in_a, in_b,
    table_sem, w_sem, own_sem, know, tile_send, tile_recv, fwd_send, row_send, row_recv,
    turn_send, turn_recv, ghost_send, ghost_recv, a_send, a_recv, b_send, b_recv,
):
    b = lax.axis_index("lat")
    s = lax.axis_index("lon")
    rows, lons, chans = field.shape
    halves = chans // LANES
    slots = ids_hbm.shape[1]
    third = weights.shape[2] // 3
    part = third // CHUNKS
    piece = part // SUB
    odd = lax.rem(b, 2)
    partner = b + 1 - 2 * odd
    s_odd = lax.rem(s, 2)
    bands = 2 * REACH + 1

    def lon_at(step):
        return lax.rem(s + step + n_lon, n_lon)

    def valid(band):
        return jnp.logical_and(band >= 0, band < n_lat)

    def place(offset):
        return (offset + REACH) * rows + 1

    def lanes(h):
        return pl.ds(h * LANES, LANES)

    far_row = 2 * third * s_odd
    near_row = 2 * third * (1 - s_odd)
    far_to = lax.rem(s + n_lon - 2 + 4 * s_odd, n_lon)
    near_to = lax.rem(s + n_lon + 1 - 2 * s_odd, n_lon)

    own_loads = [
        pltpu.make_async_copy(field.at[:, :, lanes(h)], win[h].at[pl.ds(place(0), rows)], own_sem.at[h])
        for h in range(halves)
    ]
    for copy in own_loads:
        copy.start()
    tables = [
        pltpu.make_async_copy(ids_hbm, ids, table_sem.at[0]),
        pltpu.make_async_copy(counts_hbm, counts, table_sem.at[1]),
    ]
    for table in tables:
        table.start()

    def each_peer(act):
        for offset in (-2, -1, 1, 2):
            @pl.when(valid(b + offset))
            def _():
                act(b + offset, s)
        third_band = b + 3 - 6 * odd

        @pl.when(valid(third_band))
        def _():
            act(third_band, s)
        act(b, near_to)
        act(b, lon_at(-2))
        act(b, lon_at(2))

    peers = 3 + valid(b + 3 - 6 * odd).astype(jnp.int32)
    for offset in (-2, -1, 1, 2):
        peers = peers + valid(b + offset).astype(jnp.int32)

    barrier = pltpu.get_barrier_semaphore()
    each_peer(lambda band, sector: pl.semaphore_signal(
        barrier, inc=1, device_id=(band, sector), device_id_type=MESH))

    loads = []
    for i, start in enumerate((far_row, near_row, third)):
        span = pl.ds(pl.multiple_of(start, third), third)
        loads.append(pltpu.make_async_copy(weights.at[0, 0, span], wv.at[span], w_sem.at[i]))
        loads[i].start()

    for h in range(halves):
        own_loads[h].wait()
        for r in range(rows):
            cells = win[h][place(0) + r].astype(F32)
            edge_f[0, h, pl.ds(r, 1), :] = cells[lons - 1 :]
            edge_f[1, h, pl.ds(r, 1), :] = cells[:1]
        for side in range(2):
            edge[side, h] = edge_f[side, h].astype(BF16)
    pl.semaphore_wait(barrier, peers)

    each_peer(lambda band, sector: pl.semaphore_signal(
        know, inc=1, device_id=(band, sector), device_id_type=MESH))

    def remote(src, dst, send, recv, band, sector):
        return pltpu.make_async_remote_copy(
            src_ref=src, dst_ref=dst, send_sem=send, recv_sem=recv,
            device_id=(band, sector), device_id_type=MESH,
        )

    def tile_copy(kind, h):
        delta = (partner - b, REACH, -REACH)[kind]
        return remote(
            win[h].at[pl.ds(place(0), rows)], win[h].at[pl.ds(place(-delta), rows)],
            tile_send.at[kind, h], tile_recv.at[kind, h], b + delta, s,
        )

    def forward_copy(h):
        offset = REACH - 2 * REACH * odd
        return remote(
            win[h].at[pl.ds(place(offset), rows)], win[h].at[pl.ds(place(offset + b - partner), rows)],
            fwd_send.at[h], tile_recv.at[3, h], partner, s,
        )

    def row_copy(kind, h):
        if kind == 0:
            src, dst, band = win[h].at[pl.ds(place(0) + rows - 1, 1)], win[h].at[pl.ds(0, 1)], b + REACH + 1
        else:
            src, dst, band = win[h].at[pl.ds(place(0), 1)], win[h].at[pl.ds(bands * rows + 1, 1)], b - REACH - 1
        return remote(src, dst, row_send.at[kind, h], row_recv.at[kind, h], band, s)

    def turn_copy(h):
        return remote(edge.at[1 - s_odd, h], relayed.at[h], turn_send.at[h], turn_recv.at[h], b, far_to)

    def ghost_copy(kind, h, offset):
        src, side = ((edge.at[s_odd, h], s_odd), (relayed.at[h], 1 - s_odd))[kind]
        return remote(
            src, ghost.at[side, h, pl.ds((REACH - offset) * rows, rows)],
            ghost_send.at[kind, h, offset + REACH], ghost_recv.at[kind, h, REACH - offset],
            b + offset, near_to,
        )

    def each_tile(h, act):
        for kind, delta in ((1, REACH), (2, -REACH)):
            @pl.when(valid(b + delta))
            def _():
                act(tile_copy(kind, h))
        act(tile_copy(0, h))

    def each_row(h, act):
        for kind, delta in ((0, REACH + 1), (1, -REACH - 1)):
            @pl.when(valid(b + delta))
            def _():
                act(row_copy(kind, h))

    def each_ghost(kind, h, act):
        for offset in range(-REACH, REACH + 1):
            @pl.when(valid(b + offset))
            def _():
                act(ghost_copy(kind, h, offset))

    each_tile(0, lambda copy: copy.start())
    for h in range(halves):
        turn_copy(h).start()
    pl.semaphore_wait(know, peers)
    each_ghost(0, 0, lambda copy: copy.start())
    each_row(0, lambda copy: copy.start())
    turn_copy(0).wait_recv()
    each_ghost(1, 0, lambda copy: copy.start())
    each_tile(1, lambda copy: copy.start())
    each_row(1, lambda copy: copy.start())
    each_ghost(0, 1, lambda copy: copy.start())
    turn_copy(1).wait_recv()
    each_ghost(1, 1, lambda copy: copy.start())

    forwards = valid(b + REACH - 2 * REACH * odd)
    receives = valid(b - 1 + 2 * odd)

    def pass_on(h):
        @pl.when(valid(b - REACH))
        def _():
            tile_copy(1, h).wait_recv()

        @pl.when(valid(b + REACH))
        def _():
            tile_copy(2, h).wait_recv()

        @pl.when(forwards)
        def _():
            forward_copy(h).start()

    def settle(h):
        tile_copy(0, h).wait_recv()

        @pl.when(valid(b - REACH - 1))
        def _():
            row_copy(0, h).wait_recv()

        @pl.when(valid(b + REACH + 1))
        def _():
            row_copy(1, h).wait_recv()

        for offset in range(-REACH, REACH + 1):
            @pl.when(valid(b + offset))
            def _():
                for kind in range(2):
                    ghost_copy(kind, h, -offset).wait_recv()
        for side in range(2):
            ghost_f[side, h] = ghost[side, h].astype(F32)

        @pl.when(receives)
        def _():
            forward_copy(h).wait_recv()

    first_row = place(0) - b * rows
    last_row = first_row + n_lat * rows - 1
    cell = lax.broadcasted_iota(jnp.int32, (lons, LANES), 0)
    depth = STRIP_ROWS * lons
    for table in tables:
        table.wait()
    live_count = counts[0]

    def pick(h):
        for k in range(slots):
            live = jnp.full((lons, LANES), k < live_count)
            start = ids[0, k] * STRIP_ROWS + first_row
            for j in range(STRIP_ROWS):
                at = jnp.clip(start + j, 1, bands * rows)
                centre = win[h][at].astype(F32)
                above = win[h][jnp.maximum(at - 1, first_row)].astype(F32)
                below = win[h][jnp.minimum(at + 1, last_row)].astype(F32)
                west = jnp.where(cell == 0, ghost_f[0, h, pl.ds(at - 1, 1), :], pltpu.roll(centre, 1, 0))
                east = jnp.where(cell == lons - 1, ghost_f[1, h, pl.ds(at - 1, 1), :], pltpu.roll(centre, lons - 1, 0))
                for c, value in enumerate((centre, (east - west) * 0.5, (below - above) * 0.5)):
                    span = pl.ds((3 * k + c) * depth + j * lons, lons)
                    picked[span, lanes(h)] = jnp.where(live, value, 0.0).astype(BF16)

    def product(start, i, columns):
        span = pl.ds(pl.multiple_of(start + i * part, part), part)
        return jnp.dot(wv[span, :], picked[:, columns], preferred_element_type=F32)

    def a_copy(h, j):
        return remote(out_a.at[h, j], in_a.at[h, j], a_send.at[h, j], a_recv.at[h, j], b, far_to)

    def b_copy(h, j):
        return remote(out_b.at[h, j], in_b.at[h, j], b_send.at[h, j], b_recv.at[h, j], b, near_to)

    def far(h, i):
        value = product(far_row, i, lanes(h)).astype(BF16)
        for u in range(SUB):
            out_a[h, i * SUB + u] = value[u * piece : (u + 1) * piece]
            a_copy(h, i * SUB + u).start()

    def beside(i):
        near[pl.ds(pl.multiple_of(i * part, part), part), :] = product(near_row, i, slice(None))

    def relay(h, j):
        a_copy(h, j).wait_recv()
        span = pl.ds(pl.multiple_of(j * piece, piece), piece)
        out_b[h, j] = (near[span, lanes(h)] + in_a[h, j].astype(F32)).astype(BF16)
        b_copy(h, j).start()

    def inner(i):
        own[pl.ds(pl.multiple_of(i * part, part), part), :] = product(third, i, slice(None))

    def finish(h, j):
        b_copy(h, j).wait_recv()
        span = pl.ds(pl.multiple_of(j * piece, piece), piece)
        out[span, lanes(h)] = (own[span, lanes(h)] + in_b[h, j].astype(F32)).astype(BF16)

    def steps(first, last, act):
        def step(i, carry):
            act(i)
            return carry
        lax.fori_loop(first, last, step, 0)

    def far_and_relay(i):
        far(1, i)
        relay(0, i + 1)

    def inner_and_relay(i):
        inner(i)
        relay(0, i + 1 + CHUNKS)

    def relay_and_finish(j):
        relay(1, j)
        finish(0, j)

    pass_on(0)
    settle(0)
    pick(0)
    loads[0].wait()
    steps(0, CHUNKS, functools.partial(far, 0))
    pass_on(1)
    settle(1)
    pick(1)
    loads[1].wait()
    steps(0, CHUNKS - 1, beside)
    relay(0, 0)
    beside(CHUNKS - 1)
    steps(0, CHUNKS, far_and_relay)
    loads[2].wait()
    steps(0, CHUNKS - 1, inner_and_relay)
    inner(CHUNKS - 1)
    steps(0, PIECES, relay_and_finish)
    steps(0, PIECES, functools.partial(finish, 1))

    for h in range(halves):
        turn_copy(h).wait_send()
        for kind in range(2):
            each_ghost(kind, h, lambda copy: copy.wait_send())
        each_row(h, lambda copy: copy.wait_send())
        each_tile(h, lambda copy: copy.wait_send())

        @pl.when(forwards)
        def _():
            forward_copy(h).wait_send()

        for j in range(PIECES):
            a_copy(h, j).wait_send()
            b_copy(h, j).wait_send()


def solution(mesh):
    n_lat, n_lon = mesh.shape["lat"], mesh.shape["lon"]

    def body(field, weights, strip_ids, counts):
        rows, lons, chans = field.shape
        tall, wide = weights.shape[2:]
        third = tall // 3
        piece = third // PIECES
        halves = chans // LANES
        bands = 2 * REACH + 1
        dma = pltpu.SemaphoreType.DMA
        block = (halves, PIECES, piece, LANES)
        return pl.pallas_call(
            functools.partial(kernel, n_lat, n_lon),
            out_shape=pltpu.VMEM((third, chans), BF16),
            in_specs=[
                pl.BlockSpec(memory_space=pl.ANY),
                pl.BlockSpec(memory_space=pl.ANY),
                pl.BlockSpec(memory_space=pl.ANY),
                pl.BlockSpec(memory_space=pl.ANY),
            ],
            out_specs=pl.BlockSpec(memory_space=pltpu.VMEM),
            scratch_shapes=[
                pltpu.SMEM(strip_ids.shape, jnp.int32),
                pltpu.SMEM(counts.shape, jnp.int32),
                [pltpu.VMEM((bands * rows + 2, lons, LANES), BF16) for _ in range(halves)],
                pltpu.VMEM((2, halves, rows, LANES), F32),
                pltpu.VMEM((2, halves, rows, LANES), BF16),
                pltpu.VMEM((halves, rows, LANES), BF16),
                pltpu.VMEM((2, halves, bands * rows, LANES), BF16),
                pltpu.VMEM((2, halves, bands * rows, LANES), F32),
                pltpu.VMEM((tall, wide), BF16),
                pltpu.VMEM((wide, chans), BF16),
                pltpu.VMEM((third, chans), F32),
                pltpu.VMEM((third, chans), F32),
                pltpu.VMEM(block, BF16),
                pltpu.VMEM(block, BF16),
                pltpu.VMEM(block, BF16),
                pltpu.VMEM(block, BF16),
                dma((2,)),
                dma((3,)),
                dma((halves,)),
                pltpu.SemaphoreType.REGULAR,
                dma((3, halves)),
                dma((4, halves)),
                dma((halves,)),
                dma((2, halves)),
                dma((2, halves)),
                dma((halves,)),
                dma((halves,)),
                dma((2, halves, bands)),
                dma((2, halves, bands)),
                dma((halves, PIECES)),
                dma((halves, PIECES)),
                dma((halves, PIECES)),
                dma((halves, PIECES)),
            ],
            compiler_params=pltpu.CompilerParams(collective_id=0, has_side_effects=True),
        )(field, weights, strip_ids, counts)

    placed = (P("lat", "lon", None), P("lat", "lon", None, None), P("lat", None), P("lat"))
    return jax.shard_map(
        body, mesh=mesh, in_specs=placed, out_specs=P(("lat", "lon"), None), check_vma=False
    )
```

time: 33.8 us -> 31.6 us (0.935)
  Pallas kernels: 32.2 us -> 30 us
    pallas_call x1, Pallas kernels: 32.2 us -> 30 us  [body(): pl.pallas_call(functools.partial(kernel, n_lat, n_lon), out_shape=pltpu.V...]
where the time goes in v1:
time: 31.6 us; the launch traced here: 31.5 us
  Pallas kernels  30 us (95%)
  local copies, waits for them, and re-layouts  0.8 us (3%)
  between operations  0.66 us (2%)
    pallas_call x1, Pallas kernels, body(): pl.pallas_call(functools.partial(kernel, n_lat, n_lon), out_shape=pltpu.V...  30 us
    unnamed x1, local copies, waits for them, and re-layouts  0.8 us

profile of v1, /device:TPU:0, one launch (start us, length us, event | category | flops | bytes accessed | tf_op | source)
XLA Modules:
  0.0 31.5 jit_solution(17942687731074486981)
XLA Ops:
  0.7 30.0 %shard_map.46 = bf16[1024,256]{1,0:T(8,128)(2,1)S(1)} custom-call(bf16[16,32,256]{2,1,0:T(8,128)(2,1)} %field.1, bf16[1,1,3072,3072]{3,2,1,0:T(8,128)(2,1)} %weights.1, s32[1,8]{1,0:T(1,128)} %ids_hbm.1, s32[1]{0:T(128)S(6)} %copy.7.counts_hbm), custom_call_target="tpu_custom_call" | custom-call | tf_op jit(solution)/shard_map/pallas_call | solution.py:342
  30.7 0.8 %copy.6 = bf16[1024,256]{1,0:T(8,128)(2,1)} copy(bf16[1024,256]{1,0:T(8,128)(2,1)S(1)} %shard_map.46) | data formatting | bytes 1048576

commit v2 on v1

--- a/solution.py
+++ b/solution.py
@@ -11,8 +11,6 @@
 REACH = 2
 LANES = 128
 CHUNKS = 4
-SUB = 2
-PIECES = CHUNKS * SUB
 MESH = pl.DeviceIdType.MESH
 F32 = jnp.float32
 BF16 = jnp.bfloat16
@@ -31,7 +29,6 @@
     slots = ids_hbm.shape[1]
     third = weights.shape[2] // 3
     part = third // CHUNKS
-    piece = part // SUB
     odd = lax.rem(b, 2)
     partner = b + 1 - 2 * odd
     s_odd = lax.rem(s, 2)
@@ -160,7 +157,7 @@
                 act(row_copy(kind, h))
 
     def each_ghost(kind, h, act):
-        for offset in range(-REACH, REACH + 1):
+        for offset in (-2, 2, -1, 1, 0):
             @pl.when(valid(b + offset))
             def _():
                 act(ghost_copy(kind, h, offset))
@@ -183,20 +180,27 @@
     receives = valid(b - 1 + 2 * odd)
 
     def pass_on(h):
-        @pl.when(valid(b - REACH))
-        def _():
-            tile_copy(1, h).wait_recv()
-
-        @pl.when(valid(b + REACH))
-        def _():
-            tile_copy(2, h).wait_recv()
-
         @pl.when(forwards)
         def _():
+            @pl.when(odd == 0)
+            def _():
+                tile_copy(2, h).wait_recv()
+
+            @pl.when(odd == 1)
+            def _():
+                tile_copy(1, h).wait_recv()
             forward_copy(h).start()
 
     def settle(h):
         tile_copy(0, h).wait_recv()
+
+        @pl.when(jnp.logical_and(odd == 0, valid(b - REACH)))
+        def _():
+            tile_copy(1, h).wait_recv()
+
+        @pl.when(jnp.logical_and(odd == 1, valid(b + REACH)))
+        def _():
+            tile_copy(2, h).wait_recv()
 
         @pl.when(valid(b - REACH - 1))
         def _():
@@ -245,34 +249,44 @@
         span = pl.ds(pl.multiple_of(start + i * part, part), part)
         return jnp.dot(wv[span, :], picked[:, columns], preferred_element_type=F32)
 
-    def a_copy(h, j):
-        return remote(out_a.at[h, j], in_a.at[h, j], a_send.at[h, j], a_recv.at[h, j], b, far_to)
-
-    def b_copy(h, j):
-        return remote(out_b.at[h, j], in_b.at[h, j], b_send.at[h, j], b_recv.at[h, j], b, near_to)
-
-    def far(h, i):
-        value = product(far_row, i, lanes(h)).astype(BF16)
-        for u in range(SUB):
-            out_a[h, i * SUB + u] = value[u * piece : (u + 1) * piece]
-            a_copy(h, i * SUB + u).start()
+    last = halves - 1
+    small = part // 2
+
+    def piece(i):
+        return pl.multiple_of(i * part, part), part, i
+
+    first = [(u * small, small, CHUNKS * u) for u in range(2)]
+    split = [((CHUNKS - 1) * part + u * small, small, CHUNKS - 1 + u) for u in range(2)]
+
+    def a_copy(h, piece, to=far_to):
+        span = pl.ds(piece[0], piece[1])
+        return remote(out_a.at[h, span], in_a.at[h, span], a_send.at[h, piece[2]], a_recv.at[h, piece[2]], b, to)
+
+    def b_copy(h, piece):
+        span = pl.ds(piece[0], piece[1])
+        return remote(out_b.at[h, span], in_b.at[h, span], b_send.at[h, piece[2]], b_recv.at[h, piece[2]], b, near_to)
+
+    def far(h, i, pieces=None, to=far_to):
+        out_a[h, pl.ds(pl.multiple_of(i * part, part), part)] = product(far_row, i, lanes(h)).astype(BF16)
+        for item in pieces or [piece(i)]:
+            a_copy(h, item, to).start()
 
     def beside(i):
         near[pl.ds(pl.multiple_of(i * part, part), part), :] = product(near_row, i, slice(None))
 
-    def relay(h, j):
-        a_copy(h, j).wait_recv()
-        span = pl.ds(pl.multiple_of(j * piece, piece), piece)
-        out_b[h, j] = (near[span, lanes(h)] + in_a[h, j].astype(F32)).astype(BF16)
-        b_copy(h, j).start()
+    def relay(h, piece):
+        a_copy(h, piece).wait_recv()
+        span = pl.ds(piece[0], piece[1])
+        out_b[h, span] = (near[span, lanes(h)] + in_a[h, span].astype(F32)).astype(BF16)
+        b_copy(h, piece).start()
 
     def inner(i):
         own[pl.ds(pl.multiple_of(i * part, part), part), :] = product(third, i, slice(None))
 
-    def finish(h, j):
-        b_copy(h, j).wait_recv()
-        span = pl.ds(pl.multiple_of(j * piece, piece), piece)
-        out[span, lanes(h)] = (own[span, lanes(h)] + in_b[h, j].astype(F32)).astype(BF16)
+    def finish(h, piece):
+        b_copy(h, piece).wait_recv()
+        span = pl.ds(piece[0], piece[1])
+        out[span, lanes(h)] = (own[span, lanes(h)] + in_b[h, span].astype(F32)).astype(BF16)
 
     def steps(first, last, act):
         def step(i, carry):
@@ -280,36 +294,43 @@
             return carry
         lax.fori_loop(first, last, step, 0)
 
-    def far_and_relay(i):
-        far(1, i)
-        relay(0, i + 1)
-
-    def inner_and_relay(i):
-        inner(i)
-        relay(0, i + 1 + CHUNKS)
-
-    def relay_and_finish(j):
-        relay(1, j)
-        finish(0, j)
-
     pass_on(0)
     settle(0)
     pick(0)
     loads[0].wait()
-    steps(0, CHUNKS, functools.partial(far, 0))
+    far(0, 0, first)
+    steps(1, CHUNKS, functools.partial(far, 0))
     pass_on(1)
     settle(1)
     pick(1)
     loads[1].wait()
     steps(0, CHUNKS - 1, beside)
-    relay(0, 0)
+    relay(0, first[0])
     beside(CHUNKS - 1)
-    steps(0, CHUNKS, far_and_relay)
+    relay(0, first[1])
+    steps(0, CHUNKS - 2, functools.partial(far, last))
+    relay(0, piece(1))
+    far(last, CHUNKS - 2)
+    far(last, CHUNKS - 1, split)
     loads[2].wait()
-    steps(0, CHUNKS - 1, inner_and_relay)
+    relay(0, piece(2))
+    steps(0, CHUNKS - 1, inner)
+    relay(0, piece(3))
     inner(CHUNKS - 1)
-    steps(0, PIECES, relay_and_finish)
-    steps(0, PIECES, functools.partial(finish, 1))
+    for i in range(CHUNKS - 1):
+        relay(last, piece(i))
+        if i == 0:
+            for u in range(2):
+                finish(0, first[u])
+        else:
+            finish(0, piece(i))
+    for u in range(2):
+        relay(last, split[u])
+    finish(0, piece(CHUNKS - 1))
+    for i in range(CHUNKS - 1):
+        finish(last, piece(i))
+    for u in range(2):
+        finish(last, split[u])
 
     for h in range(halves):
         turn_copy(h).wait_send()
@@ -322,9 +343,9 @@
         def _():
             forward_copy(h).wait_send()
 
-        for j in range(PIECES):
-            a_copy(h, j).wait_send()
-            b_copy(h, j).wait_send()
+        for item in (first if h == 0 else split) + [piece(i + (h == 0)) for i in range(CHUNKS - 1)]:
+            a_copy(h, item).wait_send()
+            b_copy(h, item).wait_send()
 
 
 def solution(mesh):
@@ -334,11 +355,10 @@
         rows, lons, chans = field.shape
         tall, wide = weights.shape[2:]
         third = tall // 3
-        piece = third // PIECES
         halves = chans // LANES
         bands = 2 * REACH + 1
         dma = pltpu.SemaphoreType.DMA
-        block = (halves, PIECES, piece, LANES)
+        block = (halves, third, LANES)
         return pl.pallas_call(
             functools.partial(kernel, n_lat, n_lon),
             out_shape=pltpu.VMEM((third, chans), BF16),
@@ -379,10 +399,10 @@
                 dma((halves,)),
                 dma((2, halves, bands)),
                 dma((2, halves, bands)),
-                dma((halves, PIECES)),
-                dma((halves, PIECES)),
-                dma((halves, PIECES)),
-                dma((halves, PIECES)),
+                dma((halves, CHUNKS + 1)),
+                dma((halves, CHUNKS + 1)),
+                dma((halves, CHUNKS + 1)),
+                dma((halves, CHUNKS + 1)),
             ],
             compiler_params=pltpu.CompilerParams(collective_id=0, has_side_effects=True),
         )(field, weights, strip_ids, counts)

time: 31.6 us -> 31.2 us (0.987)
  Pallas kernels: 30 us -> 29.6 us
    pallas_call x1, Pallas kernels: 30 us -> 29.6 us  [body(): pl.pallas_call(functools.partial(kernel, n_lat, n_lon), out_shape=pltpu.V...]
where the time goes in v2:
time: 31.2 us; the launch traced here: 31 us
  Pallas kernels  29.6 us (95%)
  local copies, waits for them, and re-layouts  0.8 us (3%)
  between operations  0.66 us (2%)
    pallas_call x1, Pallas kernels, body(): pl.pallas_call(functools.partial(kernel, n_lat, n_lon), out_shape=pltpu.V...  29.6 us
    unnamed x1, local copies, waits for them, and re-layouts  0.8 us

profile of v2, /device:TPU:0, one launch (start us, length us, event | category | flops | bytes accessed | tf_op | source)
XLA Modules:
  0.0 31.0 jit_solution(761518100276067660)
XLA Ops:
  0.7 29.6 %shard_map.46 = bf16[1024,256]{1,0:T(8,128)(2,1)S(1)} custom-call(bf16[16,32,256]{2,1,0:T(8,128)(2,1)} %field.1, bf16[1,1,3072,3072]{3,2,1,0:T(8,128)(2,1)} %weights.1, s32[1,8]{1,0:T(1,128)} %ids_hbm.1, s32[1]{0:T(128)S(6)} %copy.7.counts_hbm), custom_call_target="tpu_custom_call" | custom-call | tf_op jit(solution)/shard_map/pallas_call | solution.py:362
  30.3 0.8 %copy.6 = bf16[1024,256]{1,0:T(8,128)(2,1)} copy(bf16[1024,256]{1,0:T(8,128)(2,1)S(1)} %shard_map.46) | data formatting | bytes 1048576
